TPU v7x, 128 devices: a whole 4x4x4 slice. The times are simulated.
128 devices in a mesh: row: 8 (over z, core), col: 16 (over x, y).
Axes of the slice: x: 4, y: 4, z: 4, core: 2. Of those that a mesh axis runs over, the one named last changes fastest.
Arguments:
- charges: bfloat16 [256, 48, 1024], P(('row', 'col')), may hold values from -6 to 6
- near_blocks: bfloat16 [256, 2, 1024, 1024], P(('row', 'col')), may hold values from -0.125 to 0.125
- near_src: int32 [256, 2], P(('row', 'col')), may hold values from 0 to 255, as said below
- far_v: bfloat16 [128, 128, 1, 32, 1024], P(('row', 'col')), may hold values from -0.1875 to 0.1875
- far_u: bfloat16 [128, 128, 1, 32, 1024], P(('row', 'col')), may hold values from -0.125 to 0.125
- far_rank: int32 [128, 128, 1], P(('row', 'col')), may hold values from 0 to 32, as said below
- far_col: int32 [128, 128, 1], P(('row', 'col')), may hold values from 0 to 1
- far_row: int32 [128, 128, 1], P(('row', 'col')), may hold values from 0 to 1
Outputs:
- potential: float32 [256, 48, 1024], P(('row', 'col'))
Inputs may be any that keep to these rules, and one draw needn't show every extreme that they name: near_src[i, n] is a cluster of a device with the same row index as cluster i's device, whose col index differs from it by at most one, cyclically over 16. `far_rank`: in every draw some device receives only used slots (rank above 0) from every device.
All inputs are finite; a program needn't handle non-finite values.
Results may differ from a plain program's by a relative error of at most 0.0017.
Values may be sent and summed in bfloat16 or wider, within the bound.
No kernel may reach another device: no remote copies, remote signals or barrier semaphores. Data moves between devices by JAX's collectives and lax.ppermute only.
A program may use at most 128 MiB of HBM per device.

v0:
```python
import jax
import jax.numpy as jnp
from jax import lax
from jax.sharding import PartitionSpec as P


def with_halo(x, sides, width):
    for axis, dim in sides:
        devices, length = (lax.axis_size(axis), x.shape[dim])
        up = [(i, (i + 1) % devices) for i in range(devices)]
        down = [(j, i) for i, j in up]
        last = lax.slice_in_dim(x, length - width, length, axis=dim)
        first = lax.slice_in_dim(x, 0, width, axis=dim)
        before = lax.ppermute(last, axis, up)
        after = lax.ppermute(first, axis, down)
        x = jnp.concatenate([before, x, after], axis=dim)
    return x


def local(charges, near_blocks, near_src, far_v, far_u, far_rank, far_col, far_row):
    clusters_here = charges.shape[0]
    rhs_count = charges.shape[1]
    elements = charges.shape[2]
    width = far_v.shape[3]
    col_count = lax.axis_size("col")
    row_count = lax.axis_size("row")
    col_here = lax.axis_index("col")
    device_count = row_count * col_count
    slots = far_v.shape[2]
    sources = with_halo(charges, (("col", 0),), clusters_here)
    source_col = near_src // clusters_here % col_count
    position = (
        source_col - col_here + 1 + col_count
    ) % col_count * clusters_here + near_src % clusters_here
    picked = jnp.take(sources, position.reshape(-1), axis=0)
    picked = picked.reshape(clusters_here, near_src.shape[1], rhs_count, elements)
    near = jnp.einsum("lnsa,lnab->lsb", picked, near_blocks, preferred_element_type=jnp.float32)
    selected = jnp.take(charges, far_col[0].reshape(-1), axis=0)
    selected = selected.reshape(device_count, slots, rhs_count, elements)
    proj = jnp.einsum("ecsm,ecrm->ecsr", selected, far_v[0], preferred_element_type=jnp.float32)
    columns = jnp.arange(width, dtype=jnp.int32)
    keep = (columns[None, None, :] < far_rank[0][:, :, None]).astype(jnp.float32)
    coef = (proj * keep[:, :, None, :]).astype(jnp.bfloat16)
    outgoing = coef.reshape(device_count, slots, rhs_count * width)
    incoming = lax.all_to_all(outgoing, ("row", "col"), split_axis=0, concat_axis=0, tiled=True)
    incoming = incoming.reshape(device_count, slots, rhs_count, width)
    locals_here = jnp.arange(clusters_here, dtype=jnp.int32)
    onehot = (far_row[0][:, :, None] == locals_here[None, None, :]).astype(jnp.bfloat16)
    spread = incoming[:, :, None, :, :] * onehot[:, :, :, None, None]
    far = jnp.einsum("dclsr,dcrm->lsm", spread, far_u[0], preferred_element_type=jnp.float32)
    return near + far


def solution(mesh):
    return jax.shard_map(
        local,
        mesh=mesh,
        in_specs=(
            P(("row", "col"), None, None),
            P(("row", "col"), None, None, None),
            P(("row", "col"), None),
            P(("row", "col"), None, None, None, None),
            P(("row", "col"), None, None, None, None),
            P(("row", "col"), None, None),
            P(("row", "col"), None, None),
            P(("row", "col"), None, None),
        ),
        out_specs=P(("row", "col"), None, None),
        check_vma=False,
    )
```

profile of v0, /device:TPU:1, one launch (start us, length us, event | category | flops | bytes accessed | tf_op | source)
XLA Modules:
  0.0 71.2 jit_solution(5406733306202230467)
XLA Ops:
  0.0 5.7 %collective-permute-start.1 = (bf16[2,48,1024]{2,1,0:T(8,128)(2,1)}, bf16[2,48,1024]{2,1,0:T(8,128)(2,1)S(1)}, u32[]{:S(2)}, u32[]{:S(2)}) collective-permute-start(bf16[2,48,1024]{2,1,0:T(8,128)(2,1)} %param.8), channel_id=1, source_target_pairs={{1,0},{2,1},{3,2},{4,3},{5,4},{6,5},{7,6},{8,7},{9,8},{10,9},{11,1... | collective-permute-start | bytes 589832 | tf_op jit(solution)/shard_map/ppermute | solution.py:15
  5.7 0.0 collective-permute-start
  5.8 0.7 fusion.30
  6.4 0.7 compare_and_fusion
  7.1 0.0 copy-start.2
  7.1 9.0 %gather_fusion.1 = bf16[128,48,1024]{2,1,0:T(8,128)(2,1)} fusion(bf16[2,48,1024]{2,1,0:T(8,128)(2,1)} %param.8, s32[1024]{0:T(1024)S(1)} %pad_clamp_fusion), kind=kCustom, calls=%fused_computation.1 | custom fusion | bytes 25166336 | tf_op jit(solution)/shard_map/jit(_take)/gather | solution.py:38
  16.1 0.0 copy-done.2
  16.1 0.1 fusion.22
  16.2 0.0 copy-start.1
  16.2 0.0 copy-start.3
  16.2 0.0 copy-start
  16.3 8.9 %multiply_convert_fusion = bf16[128,48,32]{1,2,0:T(8,128)(2,1)S(1)} fusion(bf16[1,128,1,32,1024]{4,3,2,1,0:T(8,128)(2,1)} %param.11, bf16[128,48,1024]{2,1,0:T(8,128)(2,1)} %gather_fusion.1, pred[128]{0:T(512)(128)(4,1)S(1)} %compare_and_fusion, f32[128,32]{1,0:T(8,128)S(1)} %fusion.22), kind=kOutput, calls=%fused_computation.10 | convolution fusion | flops 409337856 | bytes 21381248 | tf_op jit(solution)/shard_map/ecsm,ecrm->ecsr/dot_general | solution.py:40
  25.1 1.4 %copy.13 = bf16[128,48,32]{0,2,1:T(8,128)(2,1)S(1)} copy(bf16[128,48,32]{1,2,0:T(8,128)(2,1)S(1)} %multiply_convert_fusion) | data formatting | bytes 786432 | tf_op jit(solution)/shard_map/convert_element_type | solution.py:43
  26.6 0.5 broadcast.142
  27.1 0.9 %reduce = bf16[128,1536]{0,1:T(8,128)(2,1)S(1)} reduce(bf16[128,1,1536]{0,2,1:T(8,128)(2,1)S(1)} %bitcast.35, bf16[]{:T(256)} %broadcast.142), dimensions={1}, to_apply=%copy.14.reduce_sub_computation | reduce | bytes 786434 | tf_op jit(solution)/shard_map/reshape | solution.py:44
  28.0 0.2 copy.26
  28.2 0.8 %reshape.177 = bf16[128,2,768]{2,1,0:T(2,128)(2,1)} reshape(bf16[128,1536]{1,0:T(8,128)(2,1)S(1)} %copy.26) | data formatting | bytes 786432
  29.1 10.6 %all-to-all-start = ((bf16[128,2,768]{2,1,0:T(2,128)(2,1)}), bf16[128,2,768]{2,1,0:T(2,128)(2,1)S(1)}, u32[]{:S(2)}, u32[]{:S(2)}) async-start(bf16[128,2,768]{2,1,0:T(2,128)(2,1)} %reshape.177), calls=%async_computation | async-start | bytes 786432 | tf_op jit(solution)/shard_map/all_to_all | solution.py:45
  39.7 0.0 copy-done.1
  39.7 0.1 reshape.154
  39.8 0.0 copy-done.3
  39.9 0.0 collective-permute-done.1
  39.9 0.0 collective-permute-done
  39.9 0.0 copy-done
  39.9 0.1 pad_maximum_fusion
  40.0 0.6 gather_fusion
  40.5 11.1 %all-to-all-done = bf16[128,2,768]{2,1,0:T(2,128)(2,1)S(1)} async-done(((bf16[128,2,768]{2,1,0:T(2,128)(2,1)}), bf16[128,2,768]{2,1,0:T(2,128)(2,1)S(1)}, u32[]{:S(2)}, u32[]{:S(2)}) %all-to-all-start) | async-done | bytes 393248 | tf_op jit(solution)/shard_map/all_to_all | solution.py:45
  51.7 0.3 reshape.178
  52.0 0.7 copy.15
  52.7 0.2 copy.16
  52.8 12.6 %fusion.12 = f32[2,48,1024]{2,1,0:T(8,128)S(1)} fusion(bf16[128,32,1024]{2,1,0:T(8,128)(2,1)} %bitcast.37, bf16[128,2]{0,1:T(2,128)(2,1)S(1)} %compare_convert_fusion, bf16[128,48,32]{0,1,2:T(8,128)(2,1)S(1)} %copy.16), kind=kOutput, calls=%fused_computation.11 | convolution fusion | flops 805699584 | bytes 9175552 | tf_op jit(solution)/shard_map/dclsr,dcrm->lsm/dot_general | solution.py:50
  65.4 5.8 %fusion.15 = f32[2,48,1024]{2,1,0:T(8,128)} fusion(f32[2,48,1024]{2,1,0:T(8,128)S(1)} %fusion.12, bf16[2,2,1024,1024]{3,2,1,0:T(8,128)(2,1)} %param.9, bf16[2,2,48,1024]{3,2,1,0:T(8,128)(2,1)S(1)} %bitcast.33, pred[2,2]{1,0:T(4,128)(4,1)S(1)} %get-tuple-element.5), kind=kOutput, calls=%fused_computation.13 | convolution fusion | flops 402948096 | bytes 9568260 | tf_op jit(solution)/shard_map/lnsa,lnab->lsb/dot_general | solution.py:37
  (5 shorter events, 0.1 us)
Async XLA Ops:
  0.0 39.9 %collective-permute-start.1 = (bf16[2,48,1024]{2,1,0:T(8,128)(2,1)}, bf16[2,48,1024]{2,1,0:T(8,128)(2,1)S(1)}, u32[]{:S(2)}, u32[]{:S(2)}) collective-permute-start(bf16[2,48,1024]{2,1,0:T(8,128)(2,1)} %param.8), channel_id=1, source_target_pairs={{1,0},{2,1},{3,2},{4,3},{5,4},{6,5},{7,6},{8,7},{9,8},{10,9},{11,1... | collective-permute-start | bytes 589832 | tf_op jit(solution)/shard_map/ppermute | solution.py:15
  5.7 34.1 %collective-permute-start = (bf16[2,48,1024]{2,1,0:T(8,128)(2,1)}, bf16[2,48,1024]{2,1,0:T(8,128)(2,1)S(1)}, u32[]{:S(2)}, u32[]{:S(2)}) collective-permute-start(bf16[2,48,1024]{2,1,0:T(8,128)(2,1)} %param.8), channel_id=1, source_target_pairs={{0,1},{1,2},{2,3},{3,4},{4,5},{5,6},{6,7},{7,8},{8,9},{9,10},{10,1... | collective-permute-start | bytes 589832 | tf_op jit(solution)/shard_map/ppermute | solution.py:14
  7.1 9.1 %copy-start.2 = (s32[1,128,1]{1,2,0:T(1,128)S(1)}, s32[1,128,1]{1,2,0:T(1,128)}, u32[]{:S(2)}) copy-start(s32[1,128,1]{1,2,0:T(1,128)} %param.13) | copy-start | bytes 1540
  16.2 23.5 %copy-start.1 = (s32[2,2]{1,0:T(2,128)S(1)}, s32[2,2]{1,0:T(2,128)}, u32[]{:S(2)}) copy-start(s32[2,2]{1,0:T(2,128)} %param.10) | copy-start | bytes 52
  16.2 23.6 %copy-start.3 = (s32[1,128,1]{1,2,0:T(1,128)S(1)}, s32[1,128,1]{1,2,0:T(1,128)}, u32[]{:S(2)}) copy-start(s32[1,128,1]{1,2,0:T(1,128)} %param.15) | copy-start | bytes 1540
  16.2 23.6 %copy-start = (bf16[2,48,1024]{2,1,0:T(8,128)(2,1)S(1)}, bf16[2,48,1024]{2,1,0:T(8,128)(2,1)}, u32[]{:S(2)}) copy-start(bf16[2,48,1024]{2,1,0:T(8,128)(2,1)} %param.8) | copy-start | bytes 589828
  29.1 22.6 %all-to-all-start = ((bf16[128,2,768]{2,1,0:T(2,128)(2,1)}), bf16[128,2,768]{2,1,0:T(2,128)(2,1)S(1)}, u32[]{:S(2)}, u32[]{:S(2)}) async-start(bf16[128,2,768]{2,1,0:T(2,128)(2,1)} %reshape.177), calls=%async_computation | async-start | bytes 786432 | tf_op jit(solution)/shard_map/all_to_all | solution.py:45
where the time goes:
time: 71.5 us; the launch traced here: 71.2 us
  matrix products  27.2 us (38%)
  starting transfers between devices  16.4 us (23%)
  local copies, waits for them, and re-layouts  13.8 us (19%)
  waiting for transfers between devices  11.1 us (16%)
  other arithmetic  2.44 us (3%)
    dot_general x1, matrix products, local(): jnp.einsum('dclsr,dcrm->lsm', spread, far_u[0], preferred_element_type=jn...  12.6 us
    all_to_all x1, waiting for transfers between devices, local(): lax.all_to_all(outgoing, ('row', 'col'), split_axis=0, concat_axis=0, til...  11.1 us
    all_to_all x1, starting transfers between devices, local(): lax.all_to_all(outgoing, ('row', 'col'), split_axis=0, concat_axis=0, til...  10.6 us
    gather x1, local copies, waits for them, and re-layouts, local(): selected = jnp.take(charges, far_col[0].reshape(-1), axis=0)  9.04 us
    dot_general x1, matrix products, local(): jnp.einsum('ecsm,ecrm->ecsr', selected, far_v[0], preferred_element_type=...  8.88 us
    dot_general x1, matrix products, local(): jnp.einsum('lnsa,lnab->lsb', picked, near_blocks, preferred_element_type=...  5.77 us
    ppermute x1, starting transfers between devices, with_halo(): after = lax.ppermute(first, axis, down)  5.75 us
    convert_element_type x1, local copies, waits for them, and re-layouts, local(): coef = (proj * keep[:, :, None, :]).astype(jnp.bfloat16)  1.44 us
  transfers between devices with their start and end apart: 3, of which 1 were waited for; matrix products, arithmetic and copies ran while one was open for 34% of the time, Pallas kernels for 0%

commit v1 on v0

v1 whole, which is shorter than its diff:
```python
import functools

import jax
import jax.numpy as jnp
from jax import lax
from jax.experimental import pallas as pl
from jax.experimental.pallas import tpu as pltpu
from jax.sharding import PartitionSpec as P

LANES = 128
V_CHUNKS = 8
N_CHUNKS = 8
STAGED = 32
U_CHUNKS = 3


def lane_pick(values, group):
    picked = values[0]
    for index in range(1, len(values)):
        picked = jnp.where(group == index, values[index], picked)
    return picked


def project_kernel(
    rank_hbm, col_hbm, charges_hbm, v_hbm, out_hbm,
    v_ref, out_ref, charges_ref, rank_ref, col_ref, sems, out_sems,
):
    blocks, width, elements = v_ref.shape
    clusters, rhs, _ = charges_ref.shape
    step = blocks // V_CHUNKS
    small = [
        pltpu.make_async_copy(charges_hbm, charges_ref, sems.at[V_CHUNKS]),
        pltpu.make_async_copy(rank_hbm, rank_ref, sems.at[V_CHUNKS + 1]),
        pltpu.make_async_copy(col_hbm, col_ref, sems.at[V_CHUNKS + 2]),
    ]
    for copy in small:
        copy.start()
    copies = []
    for chunk in range(V_CHUNKS):
        rows = pl.ds(chunk * step, step)
        copies.append(pltpu.make_async_copy(v_hbm.at[rows], v_ref.at[rows], sems.at[chunk]))
        copies[-1].start()
    per = LANES // width
    parts = rhs // 16
    lane = lax.broadcasted_iota(jnp.int32, (16, LANES), 1)
    group = lane // width
    column = lane % width
    for copy in small:
        copy.wait()
    stores = []
    x = charges_ref[...].reshape(clusters * rhs, elements)
    for chunk in range(V_CHUNKS):
        copies[chunk].wait()
        v = v_ref[pl.ds(chunk * step, step)].reshape(step * width, elements)
        proj = lax.dot_general(x, v, (((1,), (1,)), ((), ())), preferred_element_type=jnp.float32)
        for quad in range(step // per):
            first = chunk * step + quad * per
            rank = lane_pick([rank_ref[first + k] for k in range(per)], group)
            col = lane_pick([col_ref[first + k] for k in range(per)], group)
            keep = column < rank
            pieces = []
            for part in range(parts):
                at = slice(quad * LANES, (quad + 1) * LANES)
                value = proj[part * 16 : part * 16 + 16, at]
                for c in range(1, clusters):
                    start = c * rhs + part * 16
                    value = jnp.where(col == c, proj[start : start + 16, at], value)
                pieces.append(jnp.where(keep, value, 0.0))
            for k in range(per):
                message = jnp.zeros((16, LANES), jnp.float32)
                for part in range(parts):
                    shift = (part - k) * width % LANES
                    moved = pltpu.roll(pieces[part], shift, 1) if shift else pieces[part]
                    message = jnp.where(group == part, moved, message)
                out_ref[first + k] = message.astype(jnp.bfloat16)
        rows = pl.ds(chunk * step, step)
        stores.append(pltpu.make_async_copy(out_ref.at[rows], out_hbm.at[rows], out_sems.at[chunk]))
        stores[-1].start()
    for store in stores:
        store.wait()


def near_kernel(
    src_hbm, row_hbm, before_ref, mine_hbm, after_ref, b_hbm, u_hbm,
    near_ref, u_ref, lanes_ref,
    b_ref, x_ref, mine_ref, src_ref, row_ref, sems,
):
    clusters, count, elements, _ = b_ref.shape
    rhs = mine_ref.shape[1]
    last = N_CHUNKS + 1
    small = [
        pltpu.make_async_copy(src_hbm, src_ref, sems.at[last]),
        pltpu.make_async_copy(row_hbm, row_ref, sems.at[last + 1]),
        pltpu.make_async_copy(mine_hbm, mine_ref, sems.at[last + 2]),
    ]
    for copy in small:
        copy.start()
    step = elements * count * clusters // N_CHUNKS
    per = elements // step
    copies = []
    for l in range(clusters):
        for n in range(count):
            for piece in range(per):
                at = (l, n, pl.ds(piece * step, step))
                copies.append(pltpu.make_async_copy(b_hbm.at[at], b_ref.at[at], sems.at[len(copies)]))
                copies[-1].start()
    copies.append(pltpu.make_async_copy(u_hbm.at[pl.ds(0, STAGED)], u_ref, sems.at[N_CHUNKS]))
    copies[-1].start()
    for copy in small:
        copy.wait()
    width = u_ref.shape[1]
    per_row = LANES // width
    group = lax.broadcasted_iota(jnp.int32, (1, LANES), 1) // width
    for quad in range(lanes_ref.shape[0]):
        lanes_ref[quad : quad + 1] = lane_pick([row_ref[quad * per_row + k] for k in range(per_row)], group)
    cols = lax.axis_size("col")
    here = lax.axis_index("col")
    for l in range(clusters):
        for n in range(count):
            source = src_ref[l, n]
            away = lax.rem(lax.rem(source // clusters, cols) - here + 1 + cols, cols)
            which = lax.rem(source, clusters)
            value = mine_ref[which]
            value = jnp.where(away == 0, before_ref[which], value)
            value = jnp.where(away == 2, after_ref[which], value)
            x_ref[l, :, n * elements : (n + 1) * elements] = value
    for l in range(clusters):
        total = None
        for n in range(count):
            for piece in range(per):
                copies[(l * count + n) * per + piece].wait()
                start = n * elements + piece * step
                part = jnp.dot(
                    x_ref[l, :, start : start + step],
                    b_ref[l, n, piece * step : (piece + 1) * step, :],
                    preferred_element_type=jnp.float32,
                )
                total = part if total is None else total + part
        near_ref[l] = total
    copies[N_CHUNKS].wait()


def far_kernel(lanes_ref, in_ref, staged_ref, u_hbm, near_ref, out_ref, u_ref, x_ref, sems):
    kept_blocks, width, elements = staged_ref.shape
    blocks = u_ref.shape[0] // U_CHUNKS
    clusters, rhs, _ = near_ref.shape
    copies = []
    for chunk in range(U_CHUNKS):
        at = pl.ds(chunk * blocks, blocks)
        source = u_hbm.at[pl.ds(kept_blocks + chunk * blocks, blocks)]
        copies.append(pltpu.make_async_copy(source, u_ref.at[at], sems.at[chunk]))
        copies[-1].start()
    per = LANES // width
    parts = rhs // 16
    group = lax.broadcasted_iota(jnp.int32, (16, LANES), 1) // width
    spans = [(0, kept_blocks, staged_ref, 0)]
    for chunk in range(U_CHUNKS):
        spans.append((kept_blocks + chunk * blocks, blocks, u_ref, chunk * blocks))
    total = near_ref[...].reshape(clusters * rhs, elements)
    for index, (begin, size, ref, at) in enumerate(spans):
        for quad in range(begin // per, (begin + size) // per):
            first = quad * per
            row = jnp.broadcast_to(lanes_ref[quad : quad + 1], (16, LANES))
            messages = [in_ref[first + k].astype(jnp.float32) for k in range(per)]
            for part in range(parts):
                value = None
                for k in range(per):
                    shift = (k - part) * width % LANES
                    moved = pltpu.roll(messages[k], shift, 1) if shift else messages[k]
                    value = moved if value is None else jnp.where(group == k, moved, value)
                for l in range(clusters):
                    start = l * rhs + part * 16
                    kept = jnp.where(row == l, value, 0.0).astype(jnp.bfloat16)
                    x_ref[start : start + 16, quad * LANES : (quad + 1) * LANES] = kept
        if index:
            copies[index - 1].wait()
        x = x_ref[:, begin * width : (begin + size) * width]
        u = ref[pl.ds(at, size)].reshape(size * width, elements)
        total = total + jnp.dot(x, u, preferred_element_type=jnp.float32)
    out_ref[...] = total.reshape(clusters, rhs, elements)


def local(charges, near_blocks, near_src, far_v, far_u, far_rank, far_col, far_row):
    clusters, rhs, elements = charges.shape
    devices, width = far_v.shape[1], far_v.shape[3]
    count = near_src.shape[1]
    cols = lax.axis_size("col")
    vmem = pl.BlockSpec(memory_space=pltpu.VMEM)
    hbm = pl.BlockSpec(memory_space=pltpu.HBM)

    def stay(x):
        return pltpu.with_memory_space_constraint(x, pltpu.HBM)

    up = [(i, (i + 1) % cols) for i in range(cols)]
    before = lax.ppermute(charges, "col", up)
    after = lax.ppermute(charges, "col", [(j, i) for i, j in up])
    outgoing = pl.pallas_call(
        project_kernel,
        out_shape=jax.ShapeDtypeStruct((devices, 16, LANES), jnp.bfloat16),
        in_specs=[hbm] * 4,
        out_specs=hbm,
        scratch_shapes=[
            pltpu.VMEM((devices, width, elements), jnp.bfloat16),
            pltpu.VMEM((devices, 16, LANES), jnp.bfloat16),
            pltpu.VMEM(charges.shape, jnp.bfloat16),
            pltpu.SMEM((devices,), jnp.int32),
            pltpu.SMEM((devices,), jnp.int32),
            pltpu.SemaphoreType.DMA((V_CHUNKS + 3,)),
            pltpu.SemaphoreType.DMA((V_CHUNKS,)),
        ],
        compiler_params=pltpu.CompilerParams(vmem_limit_bytes=20 << 20),
        name="project",
    )(
        stay(far_rank.reshape(devices)),
        stay(far_col.reshape(devices)),
        stay(charges),
        stay(far_v.reshape(devices, width, elements)),
    )
    incoming = lax.all_to_all(outgoing, ("row", "col"), split_axis=0, concat_axis=0, tiled=True)
    u = stay(far_u.reshape(devices, width, elements))
    near, staged, lanes = pl.pallas_call(
        near_kernel,
        out_shape=(
            pltpu.VMEM(charges.shape, jnp.float32),
            pltpu.VMEM((STAGED, width, elements), jnp.bfloat16),
            pltpu.VMEM((devices * width // LANES, LANES), jnp.int32),
        ),
        in_specs=[hbm, hbm, vmem, hbm, vmem, hbm, hbm],
        out_specs=(vmem, vmem, vmem),
        scratch_shapes=[
            pltpu.VMEM(near_blocks.shape, jnp.bfloat16),
            pltpu.VMEM((clusters, rhs, count * elements), jnp.bfloat16),
            pltpu.VMEM(charges.shape, jnp.bfloat16),
            pltpu.SMEM(near_src.shape, jnp.int32),
            pltpu.SMEM((devices,), jnp.int32),
            pltpu.SemaphoreType.DMA((N_CHUNKS + 4,)),
        ],
        compiler_params=pltpu.CompilerParams(vmem_limit_bytes=24 << 20),
        cost_estimate=pl.CostEstimate(flops=20_000_000_000, bytes_accessed=10 << 20, transcendentals=0),
        name="near",
    )(
        stay(near_src),
        stay(far_row.reshape(devices)),
        before,
        stay(charges),
        after,
        stay(near_blocks),
        u,
    )
    return pl.pallas_call(
        far_kernel,
        out_shape=jax.ShapeDtypeStruct(charges.shape, jnp.float32),
        in_specs=[vmem, vmem, vmem, hbm, vmem],
        out_specs=vmem,
        scratch_shapes=[
            pltpu.VMEM((devices - STAGED, width, elements), jnp.bfloat16),
            pltpu.VMEM((clusters * rhs, devices * width), jnp.bfloat16),
            pltpu.SemaphoreType.DMA((U_CHUNKS,)),
        ],
        compiler_params=pltpu.CompilerParams(vmem_limit_bytes=24 << 20),
        name="far",
    )(lanes, incoming, staged, u, near)


def solution(mesh):
    return jax.shard_map(
        local,
        mesh=mesh,
        in_specs=(
            P(("row", "col"), None, None),
            P(("row", "col"), None, None, None),
            P(("row", "col"), None),
            P(("row", "col"), None, None, None, None),
            P(("row", "col"), None, None, None, None),
            P(("row", "col"), None, None),
            P(("row", "col"), None, None),
            P(("row", "col"), None, None),
        ),
        out_specs=P(("row", "col"), None, None),
        check_vma=False,
    )
```

time: 71.5 us -> 40.6 us (0.57)
  matrix products: 27.2 us -> 0 us
  Pallas kernels: 0 us -> 15 us
  local copies, waits for them, and re-layouts: 13.8 us -> 0 us
  other arithmetic: 2.44 us -> 0 us
  waiting for transfers between devices: 11.1 us -> 9.02 us
    dot_general x3 -> x0, matrix products: 27.2 us -> none  [the longest x1 12.6 us: local(): jnp.einsum('dclsr,dcrm->lsm', spread, far_u[0], preferred_element_type=jn...]
    pallas_call x0 -> x3, Pallas kernels: none -> 15 us  [the longest x1 6.56 us: local(): pl.pallas_call(project_kernel, out_shape=jax.ShapeDtypeStruct((devices, 1...]
    gather x2 -> x0, local copies, waits for them, and re-layouts: 9.61 us -> none  [the longest x1 9.04 us: local(): selected = jnp.take(charges, far_col[0].reshape(-1), axis=0)]
    all_to_all x1, waiting for transfers between devices: 11.1 us -> 9.01 us  [local(): lax.all_to_all(outgoing, ('row', 'col'), split_axis=0, concat_axis=0, til...]
    convert_element_type x1 -> x0, local copies, waits for them, and re-layouts: 1.44 us -> none  [local(): coef = (proj * keep[:, :, None, :]).astype(jnp.bfloat16)]
    unnamed x11 -> x0, local copies, waits for them, and re-layouts: 1.36 us -> none
    reshape x1 -> x0, other arithmetic: 0.92 us -> none  [local(): outgoing = coef.reshape(device_count, slots, rhs_count * width)]
  transfers between devices with their start and end apart: 3 -> 3, of which waited for: 1 -> 1; matrix products, arithmetic and copies ran while one was open for 34% -> 0% of each run, Pallas kernels for 0% -> 27%
where the time goes in v1:
time: 40.6 us; the launch traced here: 40.5 us
  starting transfers between devices  16.4 us (40%)
  Pallas kernels  15 us (37%)
  waiting for transfers between devices  9.02 us (22%)
    all_to_all x1, starting transfers between devices, local(): lax.all_to_all(outgoing, ('row', 'col'), split_axis=0, concat_axis=0, til...  10.6 us
    all_to_all x1, waiting for transfers between devices, local(): lax.all_to_all(outgoing, ('row', 'col'), split_axis=0, concat_axis=0, til...  9.01 us
    pallas_call x1, Pallas kernels, local(): pl.pallas_call(project_kernel, out_shape=jax.ShapeDtypeStruct((devices, 1...  6.56 us
    ppermute x1, starting transfers between devices, local(): after = lax.ppermute(charges, 'col', [(j, i) for i, j in up])  5.75 us
    pallas_call x1, Pallas kernels, local(): pl.pallas_call(near_kernel, out_shape=(pltpu.VMEM(charges.shape, jnp.floa...  4.29 us
    pallas_call x1, Pallas kernels, local(): pl.pallas_call(far_kernel, out_shape=jax.ShapeDtypeStruct(charges.shape,...  4.16 us
  transfers between devices with their start and end apart: 3, of which 1 were waited for; matrix products, arithmetic and copies ran while one was open for 0% of the time, Pallas kernels for 27%

profile of v1, /device:TPU:1, one launch (start us, length us, event | category | flops | bytes accessed | tf_op | source)
XLA Modules:
  0.0 40.5 jit_solution(9726844140363011651)
XLA Ops:
  0.0 5.7 %collective-permute-start.1 = (bf16[2,48,1024]{2,1,0:T(8,128)(2,1)}, bf16[2,48,1024]{2,1,0:T(8,128)(2,1)S(1)}, u32[]{:S(2)}, u32[]{:S(2)}) collective-permute-start(bf16[2,48,1024]{2,1,0:T(8,128)(2,1)} %charges_hbm.1), channel_id=1, source_target_pairs={{1,0},{2,1},{3,2},{4,3},{5,4},{6,5},{7,6},{8,7},{9,8},{10,9},{11,1... | collective-permute-start | bytes 589832 | tf_op jit(solution)/shard_map/ppermute | solution.py:196
  5.7 0.0 collective-permute-start
  5.8 6.6 %project.1 = bf16[128,16,128]{2,1,0:T(8,128)(2,1)} custom-call(s32[128]{0:T(128)} %bitcast.8, s32[128]{0:T(128)} %bitcast.9, bf16[2,48,1024]{2,1,0:T(8,128)(2,1)} %charges_hbm.1, bf16[128,32,1024]{2,1,0:T(8,128)(2,1)} %bitcast.5), custom_call_target="tpu_custom_call" | custom-call | tf_op jit(solution)/shard_map/project/pallas_call | solution.py:197
  12.3 10.6 %all-to-all-start = ((bf16[128,16,128]{2,1,0:T(8,128)(2,1)}), bf16[128,16,128]{2,1,0:T(8,128)(2,1)S(1)}, u32[]{:S(2)}, u32[]{:S(2)}) async-start(bf16[128,16,128]{2,1,0:T(8,128)(2,1)} %project.1), calls=%async_computation | async-start | bytes 1048576 | tf_op jit(solution)/shard_map/all_to_all | solution.py:219
  23.0 0.0 collective-permute-done.1.after_ref
  23.0 0.0 collective-permute-done.before_ref
  23.0 4.3 %near.1 = (f32[2,48,1024]{2,1,0:T(8,128)S(1)}, bf16[32,32,1024]{2,1,0:T(8,128)(2,1)S(1)}, s32[32,128]{1,0:T(8,128)S(1)}) custom-call(s32[2,2]{1,0:T(2,128)} %src_hbm.1, s32[128]{0:T(128)} %bitcast.10, bf16[2,48,1024]{2,1,0:T(8,128)(2,1)S(1)} %collective-permute-done.before_ref, bf16[2,48,1024]{2,1,0:T(8,128)(2,1)} %charges_hbm.1, ...), custom_call_target="tpu_custom_call" | custom-call | flops 20000000000 | bytes 10485760 | tf_op jit(solution)/shard_map/near/pallas_call | solution.py:221
  27.3 9.0 %all-to-all-done.in_ref = bf16[128,16,128]{2,1,0:T(8,128)(2,1)S(1)} async-done(((bf16[128,16,128]{2,1,0:T(8,128)(2,1)}), bf16[128,16,128]{2,1,0:T(8,128)(2,1)S(1)}, u32[]{:S(2)}, u32[]{:S(2)}) %all-to-all-start) | async-done | bytes 524320 | tf_op jit(solution)/shard_map/all_to_all | solution.py:219
  36.3 4.2 %far.1 = f32[2,48,1024]{2,1,0:T(8,128)} custom-call(s32[32,128]{1,0:T(8,128)S(1)} %get-tuple-element.8.lanes_ref, bf16[128,16,128]{2,1,0:T(8,128)(2,1)S(1)} %all-to-all-done.in_ref, bf16[32,32,1024]{2,1,0:T(8,128)(2,1)S(1)} %get-tuple-element.9.staged_ref, bf16[128,32,1024]{2,1,0:T(8,128)(2,1)} %bitcast.7, f32[2,48,1024]{2,1,0:T(8,128)S(1)} %get-tuple-element.10.near_ref), custom_call_target="tpu_custom_call" | custom-call | tf_op jit(solution)/shard_map/far/pallas_call | solution.py:250
Async XLA Ops:
  0.0 23.0 %collective-permute-start.1 = (bf16[2,48,1024]{2,1,0:T(8,128)(2,1)}, bf16[2,48,1024]{2,1,0:T(8,128)(2,1)S(1)}, u32[]{:S(2)}, u32[]{:S(2)}) collective-permute-start(bf16[2,48,1024]{2,1,0:T(8,128)(2,1)} %charges_hbm.1), channel_id=1, source_target_pairs={{1,0},{2,1},{3,2},{4,3},{5,4},{6,5},{7,6},{8,7},{9,8},{10,9},{11,1... | collective-permute-start | bytes 589832 | tf_op jit(solution)/shard_map/ppermute | solution.py:196
  5.7 17.2 %collective-permute-start = (bf16[2,48,1024]{2,1,0:T(8,128)(2,1)}, bf16[2,48,1024]{2,1,0:T(8,128)(2,1)S(1)}, u32[]{:S(2)}, u32[]{:S(2)}) collective-permute-start(bf16[2,48,1024]{2,1,0:T(8,128)(2,1)} %charges_hbm.1), channel_id=1, source_target_pairs={{0,1},{1,2},{2,3},{3,4},{4,5},{5,6},{6,7},{7,8},{8,9},{9,10},{10,1... | collective-permute-start | bytes 589832 | tf_op jit(solution)/shard_map/ppermute | solution.py:195
  12.3 24.0 %all-to-all-start = ((bf16[128,16,128]{2,1,0:T(8,128)(2,1)}), bf16[128,16,128]{2,1,0:T(8,128)(2,1)S(1)}, u32[]{:S(2)}, u32[]{:S(2)}) async-start(bf16[128,16,128]{2,1,0:T(8,128)(2,1)} %project.1), calls=%async_computation | async-start | bytes 1048576 | tf_op jit(solution)/shard_map/all_to_all | solution.py:219

commit v2 on v1

--- a/solution.py
+++ b/solution.py
@@ -8,10 +8,11 @@
 from jax.sharding import PartitionSpec as P
 
 LANES = 128
-V_CHUNKS = 8
+V_SIZES = (16, 32, 32, 32, 16)
 N_CHUNKS = 8
 STAGED = 32
-U_CHUNKS = 3
+U_SIZES = (40, 40, 16)
+HALVES = 2
 
 
 def lane_pick(values, group):
@@ -21,23 +22,28 @@
     return picked
 
 
+def offsets(sizes):
+    return [sum(sizes[:index]) for index in range(len(sizes))]
+
+
 def project_kernel(
     rank_hbm, col_hbm, charges_hbm, v_hbm, out_hbm,
-    v_ref, out_ref, charges_ref, rank_ref, col_ref, sems, out_sems,
+    v_ref, out_ref, charges_ref, proj_ref, rank_ref, col_ref, sems, out_sems,
 ):
-    blocks, width, elements = v_ref.shape
+    width, elements = v_ref.shape[1:]
     clusters, rhs, _ = charges_ref.shape
-    step = blocks // V_CHUNKS
+    count = len(V_SIZES)
     small = [
-        pltpu.make_async_copy(charges_hbm, charges_ref, sems.at[V_CHUNKS]),
-        pltpu.make_async_copy(rank_hbm, rank_ref, sems.at[V_CHUNKS + 1]),
-        pltpu.make_async_copy(col_hbm, col_ref, sems.at[V_CHUNKS + 2]),
+        pltpu.make_async_copy(charges_hbm, charges_ref, sems.at[count]),
+        pltpu.make_async_copy(rank_hbm, rank_ref, sems.at[count + 1]),
+        pltpu.make_async_copy(col_hbm, col_ref, sems.at[count + 2]),
     ]
     for copy in small:
         copy.start()
+    begins = offsets(V_SIZES)
     copies = []
-    for chunk in range(V_CHUNKS):
-        rows = pl.ds(chunk * step, step)
+    for chunk in range(count):
+        rows = pl.ds(begins[chunk], V_SIZES[chunk])
         copies.append(pltpu.make_async_copy(v_hbm.at[rows], v_ref.at[rows], sems.at[chunk]))
         copies[-1].start()
     per = LANES // width
@@ -47,24 +53,21 @@
     column = lane % width
     for copy in small:
         copy.wait()
-    stores = []
     x = charges_ref[...].reshape(clusters * rhs, elements)
-    for chunk in range(V_CHUNKS):
-        copies[chunk].wait()
-        v = v_ref[pl.ds(chunk * step, step)].reshape(step * width, elements)
-        proj = lax.dot_general(x, v, (((1,), (1,)), ((), ())), preferred_element_type=jnp.float32)
-        for quad in range(step // per):
-            first = chunk * step + quad * per
+
+    def pack(chunk):
+        for quad in range(V_SIZES[chunk] // per):
+            first = begins[chunk] + quad * per
             rank = lane_pick([rank_ref[first + k] for k in range(per)], group)
             col = lane_pick([col_ref[first + k] for k in range(per)], group)
             keep = column < rank
             pieces = []
             for part in range(parts):
                 at = slice(quad * LANES, (quad + 1) * LANES)
-                value = proj[part * 16 : part * 16 + 16, at]
+                value = proj_ref[chunk % 2, part * 16 : part * 16 + 16, at]
                 for c in range(1, clusters):
                     start = c * rhs + part * 16
-                    value = jnp.where(col == c, proj[start : start + 16, at], value)
+                    value = jnp.where(col == c, proj_ref[chunk % 2, start : start + 16, at], value)
                 pieces.append(jnp.where(keep, value, 0.0))
             for k in range(per):
                 message = jnp.zeros((16, LANES), jnp.float32)
@@ -73,15 +76,27 @@
                     moved = pltpu.roll(pieces[part], shift, 1) if shift else pieces[part]
                     message = jnp.where(group == part, moved, message)
                 out_ref[first + k] = message.astype(jnp.bfloat16)
-        rows = pl.ds(chunk * step, step)
+        rows = pl.ds(begins[chunk], V_SIZES[chunk])
         stores.append(pltpu.make_async_copy(out_ref.at[rows], out_hbm.at[rows], out_sems.at[chunk]))
         stores[-1].start()
+
+    stores = []
+    for chunk in range(count):
+        copies[chunk].wait()
+        size = V_SIZES[chunk]
+        v = v_ref[pl.ds(begins[chunk], size)].reshape(size * width, elements)
+        proj_ref[chunk % 2, :, : size * width] = lax.dot_general(
+            x, v, (((1,), (1,)), ((), ())), preferred_element_type=jnp.float32
+        )
+        if chunk:
+            pack(chunk - 1)
+    pack(count - 1)
     for store in stores:
         store.wait()
 
 
 def near_kernel(
-    src_hbm, row_hbm, before_ref, mine_hbm, after_ref, b_hbm, u_hbm,
+    src_hbm, row_hbm, first_ref, mine_hbm, second_ref, b_hbm, u_hbm,
     near_ref, u_ref, lanes_ref,
     b_ref, x_ref, mine_ref, src_ref, row_ref, sems,
 ):
@@ -115,14 +130,17 @@
         lanes_ref[quad : quad + 1] = lane_pick([row_ref[quad * per_row + k] for k in range(per_row)], group)
     cols = lax.axis_size("col")
     here = lax.axis_index("col")
+    even = lax.rem(here, 2) == 0
     for l in range(clusters):
         for n in range(count):
             source = src_ref[l, n]
             away = lax.rem(lax.rem(source // clusters, cols) - here + 1 + cols, cols)
             which = lax.rem(source, clusters)
             value = mine_ref[which]
-            value = jnp.where(away == 0, before_ref[which], value)
-            value = jnp.where(away == 2, after_ref[which], value)
+            from_first = away == jnp.where(even, 2, 0)
+            from_second = away == jnp.where(even, 0, 2)
+            value = jnp.where(from_first, first_ref[which], value)
+            value = jnp.where(from_second, second_ref[which], value)
             x_ref[l, :, n * elements : (n + 1) * elements] = value
     for l in range(clusters):
         total = None
@@ -140,24 +158,24 @@
     copies[N_CHUNKS].wait()
 
 
-def far_kernel(lanes_ref, in_ref, staged_ref, u_hbm, near_ref, out_ref, u_ref, x_ref, sems):
+def far_kernel(
+    lanes_ref, in_ref, staged_ref, u_hbm, near_ref, out_hbm, u_ref, x_ref, total_ref, sems, out_sems
+):
     kept_blocks, width, elements = staged_ref.shape
-    blocks = u_ref.shape[0] // U_CHUNKS
     clusters, rhs, _ = near_ref.shape
     copies = []
-    for chunk in range(U_CHUNKS):
-        at = pl.ds(chunk * blocks, blocks)
-        source = u_hbm.at[pl.ds(kept_blocks + chunk * blocks, blocks)]
-        copies.append(pltpu.make_async_copy(source, u_ref.at[at], sems.at[chunk]))
+    spans = [(0, kept_blocks, staged_ref, 0)]
+    for chunk, at in enumerate(offsets(U_SIZES)):
+        size = U_SIZES[chunk]
+        source = u_hbm.at[pl.ds(kept_blocks + at, size)]
+        copies.append(pltpu.make_async_copy(source, u_ref.at[pl.ds(at, size)], sems.at[chunk]))
         copies[-1].start()
+        spans.append((kept_blocks + at, size, u_ref, at))
     per = LANES // width
     parts = rhs // 16
     group = lax.broadcasted_iota(jnp.int32, (16, LANES), 1) // width
-    spans = [(0, kept_blocks, staged_ref, 0)]
-    for chunk in range(U_CHUNKS):
-        spans.append((kept_blocks + chunk * blocks, blocks, u_ref, chunk * blocks))
-    total = near_ref[...].reshape(clusters * rhs, elements)
-    for index, (begin, size, ref, at) in enumerate(spans):
+
+    def unpack(begin, size):
         for quad in range(begin // per, (begin + size) // per):
             first = quad * per
             row = jnp.broadcast_to(lanes_ref[quad : quad + 1], (16, LANES))
@@ -172,12 +190,29 @@
                     start = l * rhs + part * 16
                     kept = jnp.where(row == l, value, 0.0).astype(jnp.bfloat16)
                     x_ref[start : start + 16, quad * LANES : (quad + 1) * LANES] = kept
+
+    unpack(*spans[0][:2])
+    stores = []
+    for index, (begin, size, ref, at) in enumerate(spans):
         if index:
             copies[index - 1].wait()
         x = x_ref[:, begin * width : (begin + size) * width]
-        u = ref[pl.ds(at, size)].reshape(size * width, elements)
-        total = total + jnp.dot(x, u, preferred_element_type=jnp.float32)
-    out_ref[...] = total.reshape(clusters, rhs, elements)
+        final = index == len(spans) - 1
+        for half in range(HALVES):
+            columns = slice(half * (elements // HALVES), (half + 1) * (elements // HALVES))
+            u = ref[at : at + size, :, columns].reshape(size * width, elements // HALVES)
+            part = jnp.dot(x, u, preferred_element_type=jnp.float32)
+            part = part.reshape(clusters, rhs, elements // HALVES)
+            base = total_ref[:, :, columns] if index else near_ref[:, :, columns]
+            total_ref[:, :, columns] = base + part
+            if final:
+                where = (pl.ds(0, clusters), pl.ds(0, rhs), pl.ds(columns.start, elements // HALVES))
+                stores.append(pltpu.make_async_copy(total_ref.at[where], out_hbm.at[where], out_sems.at[half]))
+                stores[-1].start()
+        if not final:
+            unpack(*spans[index + 1][:2])
+    for store in stores:
+        store.wait()
 
 
 def local(charges, near_blocks, near_src, far_v, far_u, far_rank, far_col, far_row):
@@ -191,9 +226,10 @@
     def stay(x):
         return pltpu.with_memory_space_constraint(x, pltpu.HBM)
 
-    up = [(i, (i + 1) % cols) for i in range(cols)]
-    before = lax.ppermute(charges, "col", up)
-    after = lax.ppermute(charges, "col", [(j, i) for i, j in up])
+    pairs = [(i, i + 1) for i in range(0, cols, 2)]
+    others = [(i, (i + 1) % cols) for i in range(1, cols, 2)]
+    first = lax.ppermute(charges, "col", pairs + [(j, i) for i, j in pairs])
+    second = lax.ppermute(charges, "col", others + [(j, i) for i, j in others])
     outgoing = pl.pallas_call(
         project_kernel,
         out_shape=jax.ShapeDtypeStruct((devices, 16, LANES), jnp.bfloat16),
@@ -203,10 +239,11 @@
             pltpu.VMEM((devices, width, elements), jnp.bfloat16),
             pltpu.VMEM((devices, 16, LANES), jnp.bfloat16),
             pltpu.VMEM(charges.shape, jnp.bfloat16),
+            pltpu.VMEM((2, clusters * rhs, max(V_SIZES) * width), jnp.float32),
             pltpu.SMEM((devices,), jnp.int32),
             pltpu.SMEM((devices,), jnp.int32),
-            pltpu.SemaphoreType.DMA((V_CHUNKS + 3,)),
-            pltpu.SemaphoreType.DMA((V_CHUNKS,)),
+            pltpu.SemaphoreType.DMA((len(V_SIZES) + 3,)),
+            pltpu.SemaphoreType.DMA((len(V_SIZES),)),
         ],
         compiler_params=pltpu.CompilerParams(vmem_limit_bytes=20 << 20),
         name="project",
@@ -241,9 +278,9 @@
     )(
         stay(near_src),
         stay(far_row.reshape(devices)),
-        before,
+        first,
         stay(charges),
-        after,
+        second,
         stay(near_blocks),
         u,
     )
@@ -251,11 +288,13 @@
         far_kernel,
         out_shape=jax.ShapeDtypeStruct(charges.shape, jnp.float32),
         in_specs=[vmem, vmem, vmem, hbm, vmem],
-        out_specs=vmem,
+        out_specs=hbm,
         scratch_shapes=[
             pltpu.VMEM((devices - STAGED, width, elements), jnp.bfloat16),
             pltpu.VMEM((clusters * rhs, devices * width), jnp.bfloat16),
-            pltpu.SemaphoreType.DMA((U_CHUNKS,)),
+            pltpu.VMEM(charges.shape, jnp.float32),
+            pltpu.SemaphoreType.DMA((len(U_SIZES),)),
+            pltpu.SemaphoreType.DMA((HALVES,)),
         ],
         compiler_params=pltpu.CompilerParams(vmem_limit_bytes=24 << 20),
         name="far",

time: 40.6 us -> 36.9 us (0.909)
  starting transfers between devices: 16.4 us -> 13.6 us
  Pallas kernels: 15 us -> 14.1 us
    all_to_all x1, starting transfers between devices: 10.6 us -> 7.89 us  [local(): lax.all_to_all(outgoing, ('row', 'col'), split_axis=0, concat_axis=0, til...]
    pallas_call x1, Pallas kernels: 6.56 us -> 5.65 us  [local(): pl.pallas_call(project_kernel, out_shape=jax.ShapeDtypeStruct((devices, 1...]
where the time goes in v2:
time: 36.9 us; the launch traced here: 36.8 us
  Pallas kernels  14.1 us (38%)
  starting transfers between devices  13.6 us (37%)
  waiting for transfers between devices  9.02 us (24%)
    all_to_all x1, waiting for transfers between devices, local(): lax.all_to_all(outgoing, ('row', 'col'), split_axis=0, concat_axis=0, til...  9.01 us
    all_to_all x1, starting transfers between devices, local(): lax.all_to_all(outgoing, ('row', 'col'), split_axis=0, concat_axis=0, til...  7.89 us
    ppermute x1, starting transfers between devices, local(): second = lax.ppermute(charges, 'col', others + [(j, i) for i, j in others])  5.75 us
    pallas_call x1, Pallas kernels, local(): pl.pallas_call(project_kernel, out_shape=jax.ShapeDtypeStruct((devices, 1...  5.65 us
    pallas_call x1, Pallas kernels, local(): pl.pallas_call(near_kernel, out_shape=(pltpu.VMEM(charges.shape, jnp.floa...  4.29 us
    pallas_call x1, Pallas kernels, local(): pl.pallas_call(far_kernel, out_shape=jax.ShapeDtypeStruct(charges.shape,...  4.12 us
  transfers between devices with their start and end apart: 3, of which 1 were waited for; matrix products, arithmetic and copies ran while one was open for 0% of the time, Pallas kernels for 27%

profile of v2, /device:TPU:1, one launch (start us, length us, event | category | flops | bytes accessed | tf_op | source)
XLA Modules:
  0.0 36.8 jit_solution(15140391655282367331)
XLA Ops:
  0.0 5.7 %collective-permute-start.1 = (bf16[2,48,1024]{2,1,0:T(8,128)(2,1)}, bf16[2,48,1024]{2,1,0:T(8,128)(2,1)S(1)}, u32[]{:S(2)}, u32[]{:S(2)}) collective-permute-start(bf16[2,48,1024]{2,1,0:T(8,128)(2,1)} %charges_hbm.1), channel_id=1, source_target_pairs={{1,2},{3,4},{5,6},{7,8},{9,10},{11,12},{13,14},{15,0},{2,1},{4,3},... | collective-permute-start | bytes 589832 | tf_op jit(solution)/shard_map/ppermute | solution.py:232
  5.7 0.0 collective-permute-start
  5.8 5.7 %project.1 = bf16[128,16,128]{2,1,0:T(8,128)(2,1)} custom-call(s32[128]{0:T(128)} %bitcast.8, s32[128]{0:T(128)} %bitcast.9, bf16[2,48,1024]{2,1,0:T(8,128)(2,1)} %charges_hbm.1, bf16[128,32,1024]{2,1,0:T(8,128)(2,1)} %bitcast.5), custom_call_target="tpu_custom_call" | custom-call | tf_op jit(solution)/shard_map/project/pallas_call | solution.py:233
  11.4 7.9 %all-to-all-start = ((bf16[128,16,128]{2,1,0:T(8,128)(2,1)}), bf16[128,16,128]{2,1,0:T(8,128)(2,1)S(1)}, u32[]{:S(2)}, u32[]{:S(2)}) async-start(bf16[128,16,128]{2,1,0:T(8,128)(2,1)} %project.1), calls=%async_computation | async-start | bytes 1048576 | tf_op jit(solution)/shard_map/all_to_all | solution.py:256
  19.3 0.0 collective-permute-done.1.second_ref
  19.3 0.0 collective-permute-done.first_ref
  19.3 4.3 %near.1 = (f32[2,48,1024]{2,1,0:T(8,128)S(1)}, bf16[32,32,1024]{2,1,0:T(8,128)(2,1)S(1)}, s32[32,128]{1,0:T(8,128)S(1)}) custom-call(s32[2,2]{1,0:T(2,128)} %src_hbm.1, s32[128]{0:T(128)} %bitcast.10, bf16[2,48,1024]{2,1,0:T(8,128)(2,1)S(1)} %collective-permute-done.first_ref, bf16[2,48,1024]{2,1,0:T(8,128)(2,1)} %charges_hbm.1, ...), custom_call_target="tpu_custom_call" | custom-call | flops 20000000000 | bytes 10485760 | tf_op jit(solution)/shard_map/near/pallas_call | solution.py:258
  23.6 9.0 %all-to-all-done.in_ref = bf16[128,16,128]{2,1,0:T(8,128)(2,1)S(1)} async-done(((bf16[128,16,128]{2,1,0:T(8,128)(2,1)}), bf16[128,16,128]{2,1,0:T(8,128)(2,1)S(1)}, u32[]{:S(2)}, u32[]{:S(2)}) %all-to-all-start) | async-done | bytes 524320 | tf_op jit(solution)/shard_map/all_to_all | solution.py:256
  32.6 4.1 %far.1 = f32[2,48,1024]{2,1,0:T(8,128)} custom-call(s32[32,128]{1,0:T(8,128)S(1)} %get-tuple-element.8.lanes_ref, bf16[128,16,128]{2,1,0:T(8,128)(2,1)S(1)} %all-to-all-done.in_ref, bf16[32,32,1024]{2,1,0:T(8,128)(2,1)S(1)} %get-tuple-element.9.staged_ref, bf16[128,32,1024]{2,1,0:T(8,128)(2,1)} %bitcast.7, f32[2,48,1024]{2,1,0:T(8,128)S(1)} %get-tuple-element.10.near_ref), custom_call_target="tpu_custom_call" | custom-call | tf_op jit(solution)/shard_map/far/pallas_call | solution.py:287
Async XLA Ops:
  0.0 19.3 %collective-permute-start.1 = (bf16[2,48,1024]{2,1,0:T(8,128)(2,1)}, bf16[2,48,1024]{2,1,0:T(8,128)(2,1)S(1)}, u32[]{:S(2)}, u32[]{:S(2)}) collective-permute-start(bf16[2,48,1024]{2,1,0:T(8,128)(2,1)} %charges_hbm.1), channel_id=1, source_target_pairs={{1,2},{3,4},{5,6},{7,8},{9,10},{11,12},{13,14},{15,0},{2,1},{4,3},... | collective-permute-start | bytes 589832 | tf_op jit(solution)/shard_map/ppermute | solution.py:232
  5.7 13.6 %collective-permute-start = (bf16[2,48,1024]{2,1,0:T(8,128)(2,1)}, bf16[2,48,1024]{2,1,0:T(8,128)(2,1)S(1)}, u32[]{:S(2)}, u32[]{:S(2)}) collective-permute-start(bf16[2,48,1024]{2,1,0:T(8,128)(2,1)} %charges_hbm.1), channel_id=1, source_target_pairs={{0,1},{2,3},{4,5},{6,7},{8,9},{10,11},{12,13},{14,15},{1,0},{3,2},... | collective-permute-start | bytes 589832 | tf_op jit(solution)/shard_map/ppermute | solution.py:231
  11.4 21.2 %all-to-all-start = ((bf16[128,16,128]{2,1,0:T(8,128)(2,1)}), bf16[128,16,128]{2,1,0:T(8,128)(2,1)S(1)}, u32[]{:S(2)}, u32[]{:S(2)}) async-start(bf16[128,16,128]{2,1,0:T(8,128)(2,1)} %project.1), calls=%async_computation | async-start | bytes 1048576 | tf_op jit(solution)/shard_map/all_to_all | solution.py:256

commit v3 on v2

--- a/solution.py
+++ b/solution.py
@@ -20,6 +20,19 @@
     for index in range(1, len(values)):
         picked = jnp.where(group == index, values[index], picked)
     return picked
+
+
+def block_transpose(tile, width):
+    per = LANES // width
+    rows = tile.shape[0] // per
+    across = lax.broadcasted_iota(jnp.int32, tile.shape, 1) // width
+    down = lax.broadcasted_iota(jnp.int32, tile.shape, 0) // rows
+    away = lax.rem(across - down + per, per)
+    result = tile
+    for k in range(1, per):
+        moved = pltpu.roll(pltpu.roll(tile, width * k, 1), tile.shape[0] - rows * k, 0)
+        result = jnp.where(away == k, moved, result)
+    return result
 
 
 def offsets(sizes):
@@ -61,21 +74,16 @@
             rank = lane_pick([rank_ref[first + k] for k in range(per)], group)
             col = lane_pick([col_ref[first + k] for k in range(per)], group)
             keep = column < rank
-            pieces = []
+            at = slice(quad * LANES, (quad + 1) * LANES)
             for part in range(parts):
-                at = slice(quad * LANES, (quad + 1) * LANES)
                 value = proj_ref[chunk % 2, part * 16 : part * 16 + 16, at]
                 for c in range(1, clusters):
                     start = c * rhs + part * 16
                     value = jnp.where(col == c, proj_ref[chunk % 2, start : start + 16, at], value)
-                pieces.append(jnp.where(keep, value, 0.0))
-            for k in range(per):
-                message = jnp.zeros((16, LANES), jnp.float32)
-                for part in range(parts):
-                    shift = (part - k) * width % LANES
-                    moved = pltpu.roll(pieces[part], shift, 1) if shift else pieces[part]
-                    message = jnp.where(group == part, moved, message)
-                out_ref[first + k] = message.astype(jnp.bfloat16)
+                value = jnp.where(keep, value, 0.0).astype(jnp.bfloat16)
+                value = block_transpose(value, width)
+                for k in range(per):
+                    out_ref[first + k, part] = value[k * 16 // per : (k + 1) * 16 // per]
         rows = pl.ds(begins[chunk], V_SIZES[chunk])
         stores.append(pltpu.make_async_copy(out_ref.at[rows], out_hbm.at[rows], out_sems.at[chunk]))
         stores[-1].start()
@@ -127,7 +135,8 @@
     per_row = LANES // width
     group = lax.broadcasted_iota(jnp.int32, (1, LANES), 1) // width
     for quad in range(lanes_ref.shape[0]):
-        lanes_ref[quad : quad + 1] = lane_pick([row_ref[quad * per_row + k] for k in range(per_row)], group)
+        row = lane_pick([row_ref[quad * per_row + k] for k in range(per_row)], group)
+        lanes_ref[quad : quad + 1] = row.astype(jnp.float32)
     cols = lax.axis_size("col")
     here = lax.axis_index("col")
     even = lax.rem(here, 2) == 0
@@ -173,22 +182,17 @@
         spans.append((kept_blocks + at, size, u_ref, at))
     per = LANES // width
     parts = rhs // 16
-    group = lax.broadcasted_iota(jnp.int32, (16, LANES), 1) // width
 
     def unpack(begin, size):
         for quad in range(begin // per, (begin + size) // per):
             first = quad * per
-            row = jnp.broadcast_to(lanes_ref[quad : quad + 1], (16, LANES))
-            messages = [in_ref[first + k].astype(jnp.float32) for k in range(per)]
+            row = jnp.broadcast_to(lanes_ref[quad : quad + 1], (16, LANES)).astype(jnp.bfloat16)
             for part in range(parts):
-                value = None
-                for k in range(per):
-                    shift = (k - part) * width % LANES
-                    moved = pltpu.roll(messages[k], shift, 1) if shift else messages[k]
-                    value = moved if value is None else jnp.where(group == k, moved, value)
+                value = jnp.concatenate([in_ref[first + k, part] for k in range(per)], axis=0)
+                value = block_transpose(value, width)
                 for l in range(clusters):
                     start = l * rhs + part * 16
-                    kept = jnp.where(row == l, value, 0.0).astype(jnp.bfloat16)
+                    kept = jnp.where(row == l, value, jnp.zeros_like(value))
                     x_ref[start : start + 16, quad * LANES : (quad + 1) * LANES] = kept
 
     unpack(*spans[0][:2])
@@ -219,6 +223,8 @@
     clusters, rhs, elements = charges.shape
     devices, width = far_v.shape[1], far_v.shape[3]
     count = near_src.shape[1]
+    per = LANES // width
+    message = (devices, rhs // 16, 16 // per, LANES)
     cols = lax.axis_size("col")
     vmem = pl.BlockSpec(memory_space=pltpu.VMEM)
     hbm = pl.BlockSpec(memory_space=pltpu.HBM)
@@ -232,12 +238,12 @@
     second = lax.ppermute(charges, "col", others + [(j, i) for i, j in others])
     outgoing = pl.pallas_call(
         project_kernel,
-        out_shape=jax.ShapeDtypeStruct((devices, 16, LANES), jnp.bfloat16),
+        out_shape=jax.ShapeDtypeStruct(message, jnp.bfloat16),
         in_specs=[hbm] * 4,
         out_specs=hbm,
         scratch_shapes=[
             pltpu.VMEM((devices, width, elements), jnp.bfloat16),
-            pltpu.VMEM((devices, 16, LANES), jnp.bfloat16),
+            pltpu.VMEM(message, jnp.bfloat16),
             pltpu.VMEM(charges.shape, jnp.bfloat16),
             pltpu.VMEM((2, clusters * rhs, max(V_SIZES) * width), jnp.float32),
             pltpu.SMEM((devices,), jnp.int32),
@@ -260,7 +266,7 @@
         out_shape=(
             pltpu.VMEM(charges.shape, jnp.float32),
             pltpu.VMEM((STAGED, width, elements), jnp.bfloat16),
-            pltpu.VMEM((devices * width // LANES, LANES), jnp.int32),
+            pltpu.VMEM((devices * width // LANES, LANES), jnp.float32),
         ),
         in_specs=[hbm, hbm, vmem, hbm, vmem, hbm, hbm],
         out_specs=(vmem, vmem, vmem),

time: 36.9 us -> 35.6 us (0.965)
  waiting for transfers between devices: 9.02 us -> 7.68 us
    all_to_all x1, waiting for transfers between devices: 9.01 us -> 7.68 us  [local(): lax.all_to_all(outgoing, ('row', 'col'), split_axis=0, concat_axis=0, til...]
  transfers between devices with their start and end apart: 3 -> 3, of which waited for: 1 -> 1; matrix products, arithmetic and copies ran while one was open for 0% -> 0% of each run, Pallas kernels for 27% -> 28%
where the time goes in v3:
time: 35.6 us; the launch traced here: 35.4 us
  Pallas kernels  14.1 us (40%)
  starting transfers between devices  13.6 us (38%)
  waiting for transfers between devices  7.68 us (22%)
    all_to_all x1, starting transfers between devices, local(): lax.all_to_all(outgoing, ('row', 'col'), split_axis=0, concat_axis=0, til...  7.89 us
    all_to_all x1, waiting for transfers between devices, local(): lax.all_to_all(outgoing, ('row', 'col'), split_axis=0, concat_axis=0, til...  7.68 us
    ppermute x1, starting transfers between devices, local(): second = lax.ppermute(charges, 'col', others + [(j, i) for i, j in others])  5.75 us
    pallas_call x1, Pallas kernels, local(): pl.pallas_call(project_kernel, out_shape=jax.ShapeDtypeStruct(message, jn...  5.65 us
    pallas_call x1, Pallas kernels, local(): pl.pallas_call(near_kernel, out_shape=(pltpu.VMEM(charges.shape, jnp.floa...  4.29 us
    pallas_call x1, Pallas kernels, local(): pl.pallas_call(far_kernel, out_shape=jax.ShapeDtypeStruct(charges.shape,...  4.13 us
  transfers between devices with their start and end apart: 3, of which 1 were waited for; matrix products, arithmetic and copies ran while one was open for 0% of the time, Pallas kernels for 28%

profile of v3, /device:TPU:1, one launch (start us, length us, event | category | flops | bytes accessed | tf_op | source)
XLA Modules:
  0.0 35.4 jit_solution(2860527564759351176)
XLA Ops:
  0.0 5.7 %collective-permute-start.1 = (bf16[2,48,1024]{2,1,0:T(8,128)(2,1)}, bf16[2,48,1024]{2,1,0:T(8,128)(2,1)S(1)}, u32[]{:S(2)}, u32[]{:S(2)}) collective-permute-start(bf16[2,48,1024]{2,1,0:T(8,128)(2,1)} %charges_hbm.1), channel_id=1, source_target_pairs={{1,2},{3,4},{5,6},{7,8},{9,10},{11,12},{13,14},{15,0},{2,1},{4,3},... | collective-permute-start | bytes 589832 | tf_op jit(solution)/shard_map/ppermute | solution.py:238
  5.7 0.0 collective-permute-start
  5.8 5.7 %project.1 = bf16[128,3,4,128]{3,2,1,0:T(4,128)(2,1)} custom-call(s32[128]{0:T(128)} %bitcast.8, s32[128]{0:T(128)} %bitcast.9, bf16[2,48,1024]{2,1,0:T(8,128)(2,1)} %charges_hbm.1, bf16[128,32,1024]{2,1,0:T(8,128)(2,1)} %bitcast.5), custom_call_target="tpu_custom_call" | custom-call | tf_op jit(solution)/shard_map/project/pallas_call | solution.py:239
  11.4 7.9 %all-to-all-start = ((bf16[128,3,4,128]{3,2,1,0:T(4,128)(2,1)}), bf16[128,3,4,128]{3,2,1,0:T(4,128)(2,1)S(1)}, u32[]{:S(2)}, u32[]{:S(2)}) async-start(bf16[128,3,4,128]{3,2,1,0:T(4,128)(2,1)} %project.1), calls=%async_computation | async-start | bytes 786432 | tf_op jit(solution)/shard_map/all_to_all | solution.py:262
  19.3 0.0 collective-permute-done.1.second_ref
  19.3 0.0 collective-permute-done.first_ref
  19.3 4.3 %near.1 = (f32[2,48,1024]{2,1,0:T(8,128)S(1)}, bf16[32,32,1024]{2,1,0:T(8,128)(2,1)S(1)}, f32[32,128]{1,0:T(8,128)S(1)}) custom-call(s32[2,2]{1,0:T(2,128)} %src_hbm.1, s32[128]{0:T(128)} %bitcast.10, bf16[2,48,1024]{2,1,0:T(8,128)(2,1)S(1)} %collective-permute-done.first_ref, bf16[2,48,1024]{2,1,0:T(8,128)(2,1)} %charges_hbm.1, ...), custom_call_target="tpu_custom_call" | custom-call | flops 20000000000 | bytes 10485760 | tf_op jit(solution)/shard_map/near/pallas_call | solution.py:264
  23.6 7.7 %all-to-all-done.in_ref = bf16[128,3,4,128]{3,2,1,0:T(4,128)(2,1)S(1)} async-done(((bf16[128,3,4,128]{3,2,1,0:T(4,128)(2,1)}), bf16[128,3,4,128]{3,2,1,0:T(4,128)(2,1)S(1)}, u32[]{:S(2)}, u32[]{:S(2)}) %all-to-all-start) | async-done | bytes 393248 | tf_op jit(solution)/shard_map/all_to_all | solution.py:262
  31.3 4.1 %far.1 = f32[2,48,1024]{2,1,0:T(8,128)} custom-call(f32[32,128]{1,0:T(8,128)S(1)} %get-tuple-element.8.lanes_ref, bf16[128,3,4,128]{3,2,1,0:T(4,128)(2,1)S(1)} %all-to-all-done.in_ref, bf16[32,32,1024]{2,1,0:T(8,128)(2,1)S(1)} %get-tuple-element.9.staged_ref, bf16[128,32,1024]{2,1,0:T(8,128)(2,1)} %bitcast.7, f32[2,48,1024]{2,1,0:T(8,128)S(1)} %get-tuple-element.10.near_ref), custom_call_target="tpu_custom_call" | custom-call | tf_op jit(solution)/shard_map/far/pallas_call | solution.py:293
Async XLA Ops:
  0.0 19.3 %collective-permute-start.1 = (bf16[2,48,1024]{2,1,0:T(8,128)(2,1)}, bf16[2,48,1024]{2,1,0:T(8,128)(2,1)S(1)}, u32[]{:S(2)}, u32[]{:S(2)}) collective-permute-start(bf16[2,48,1024]{2,1,0:T(8,128)(2,1)} %charges_hbm.1), channel_id=1, source_target_pairs={{1,2},{3,4},{5,6},{7,8},{9,10},{11,12},{13,14},{15,0},{2,1},{4,3},... | collective-permute-start | bytes 589832 | tf_op jit(solution)/shard_map/ppermute | solution.py:238
  5.7 13.6 %collective-permute-start = (bf16[2,48,1024]{2,1,0:T(8,128)(2,1)}, bf16[2,48,1024]{2,1,0:T(8,128)(2,1)S(1)}, u32[]{:S(2)}, u32[]{:S(2)}) collective-permute-start(bf16[2,48,1024]{2,1,0:T(8,128)(2,1)} %charges_hbm.1), channel_id=1, source_target_pairs={{0,1},{2,3},{4,5},{6,7},{8,9},{10,11},{12,13},{14,15},{1,0},{3,2},... | collective-permute-start | bytes 589832 | tf_op jit(solution)/shard_map/ppermute | solution.py:237
  11.4 19.9 %all-to-all-start = ((bf16[128,3,4,128]{3,2,1,0:T(4,128)(2,1)}), bf16[128,3,4,128]{3,2,1,0:T(4,128)(2,1)S(1)}, u32[]{:S(2)}, u32[]{:S(2)}) async-start(bf16[128,3,4,128]{3,2,1,0:T(4,128)(2,1)} %project.1), calls=%async_computation | async-start | bytes 786432 | tf_op jit(solution)/shard_map/all_to_all | solution.py:262

commit v4 on v3

--- a/solution.py
+++ b/solution.py
@@ -10,9 +10,9 @@
 LANES = 128
 V_SIZES = (16, 32, 32, 32, 16)
 N_CHUNKS = 8
-STAGED = 32
-U_SIZES = (40, 40, 16)
-HALVES = 2
+STAGED = 40
+U_SIZES = (16, 16, 16, 16, 16, 8)
+HALVES = 1
 
 
 def lane_pick(values, group):
@@ -105,8 +105,8 @@
 
 def near_kernel(
     src_hbm, row_hbm, first_ref, mine_hbm, second_ref, b_hbm, u_hbm,
-    near_ref, u_ref, lanes_ref,
-    b_ref, x_ref, mine_ref, src_ref, row_ref, sems,
+    near_hbm, u_ref, lanes_ref,
+    b_ref, x_ref, near_ref, mine_ref, src_ref, row_ref, sems,
 ):
     clusters, count, elements, _ = b_ref.shape
     rhs = mine_ref.shape[1]
@@ -151,6 +151,7 @@
             value = jnp.where(from_first, first_ref[which], value)
             value = jnp.where(from_second, second_ref[which], value)
             x_ref[l, :, n * elements : (n + 1) * elements] = value
+    stores = []
     for l in range(clusters):
         total = None
         for n in range(count):
@@ -164,14 +165,20 @@
                 )
                 total = part if total is None else total + part
         near_ref[l] = total
+        stores.append(pltpu.make_async_copy(near_ref.at[l], near_hbm.at[l], sems.at[last + 3 + l]))
+        stores[-1].start()
     copies[N_CHUNKS].wait()
+    for store in stores:
+        store.wait()
 
 
 def far_kernel(
-    lanes_ref, in_ref, staged_ref, u_hbm, near_ref, out_hbm, u_ref, x_ref, total_ref, sems, out_sems
+    lanes_ref, in_ref, staged_ref, u_hbm, near_hbm, out_hbm, u_ref, x_ref, total_ref, near_ref, sems, out_sems
 ):
     kept_blocks, width, elements = staged_ref.shape
-    clusters, rhs, _ = near_ref.shape
+    clusters, rhs, _ = total_ref.shape
+    fetch = pltpu.make_async_copy(near_hbm, near_ref, sems.at[len(U_SIZES)])
+    fetch.start()
     copies = []
     spans = [(0, kept_blocks, staged_ref, 0)]
     for chunk, at in enumerate(offsets(U_SIZES)):
@@ -200,6 +207,8 @@
     for index, (begin, size, ref, at) in enumerate(spans):
         if index:
             copies[index - 1].wait()
+        if index == 1:
+            fetch.wait()
         x = x_ref[:, begin * width : (begin + size) * width]
         final = index == len(spans) - 1
         for half in range(HALVES):
@@ -207,8 +216,11 @@
             u = ref[at : at + size, :, columns].reshape(size * width, elements // HALVES)
             part = jnp.dot(x, u, preferred_element_type=jnp.float32)
             part = part.reshape(clusters, rhs, elements // HALVES)
-            base = total_ref[:, :, columns] if index else near_ref[:, :, columns]
-            total_ref[:, :, columns] = base + part
+            if index:
+                part += total_ref[:, :, columns]
+            if index == 1:
+                part += near_ref[:, :, columns]
+            total_ref[:, :, columns] = part
             if final:
                 where = (pl.ds(0, clusters), pl.ds(0, rhs), pl.ds(columns.start, elements // HALVES))
                 stores.append(pltpu.make_async_copy(total_ref.at[where], out_hbm.at[where], out_sems.at[half]))
@@ -264,19 +276,20 @@
     near, staged, lanes = pl.pallas_call(
         near_kernel,
         out_shape=(
-            pltpu.VMEM(charges.shape, jnp.float32),
+            pltpu.HBM(charges.shape, jnp.float32),
             pltpu.VMEM((STAGED, width, elements), jnp.bfloat16),
             pltpu.VMEM((devices * width // LANES, LANES), jnp.float32),
         ),
         in_specs=[hbm, hbm, vmem, hbm, vmem, hbm, hbm],
-        out_specs=(vmem, vmem, vmem),
+        out_specs=(hbm, vmem, vmem),
         scratch_shapes=[
             pltpu.VMEM(near_blocks.shape, jnp.bfloat16),
             pltpu.VMEM((clusters, rhs, count * elements), jnp.bfloat16),
+            pltpu.VMEM(charges.shape, jnp.float32),
             pltpu.VMEM(charges.shape, jnp.bfloat16),
             pltpu.SMEM(near_src.shape, jnp.int32),
             pltpu.SMEM((devices,), jnp.int32),
-            pltpu.SemaphoreType.DMA((N_CHUNKS + 4,)),
+            pltpu.SemaphoreType.DMA((N_CHUNKS + 4 + clusters,)),
         ],
         compiler_params=pltpu.CompilerParams(vmem_limit_bytes=24 << 20),
         cost_estimate=pl.CostEstimate(flops=20_000_000_000, bytes_accessed=10 << 20, transcendentals=0),
@@ -293,18 +306,19 @@
     return pl.pallas_call(
         far_kernel,
         out_shape=jax.ShapeDtypeStruct(charges.shape, jnp.float32),
-        in_specs=[vmem, vmem, vmem, hbm, vmem],
+        in_specs=[vmem, vmem, vmem, hbm, hbm],
         out_specs=hbm,
         scratch_shapes=[
             pltpu.VMEM((devices - STAGED, width, elements), jnp.bfloat16),
             pltpu.VMEM((clusters * rhs, devices * width), jnp.bfloat16),
             pltpu.VMEM(charges.shape, jnp.float32),
-            pltpu.SemaphoreType.DMA((len(U_SIZES),)),
+            pltpu.VMEM(charges.shape, jnp.float32),
+            pltpu.SemaphoreType.DMA((len(U_SIZES) + 1,)),
             pltpu.SemaphoreType.DMA((HALVES,)),
         ],
         compiler_params=pltpu.CompilerParams(vmem_limit_bytes=24 << 20),
         name="far",
-    )(lanes, incoming, staged, u, near)
+    )(lanes, incoming, staged, u, stay(near))
 
 
 def solution(mesh):

time: 35.6 us -> 35.3 us (level)
  transfers between devices with their start and end apart: 3 -> 3, of which waited for: 1 -> 1; matrix products, arithmetic and copies ran while one was open for 0% -> 0% of each run, Pallas kernels for 28% -> 29%
where the time goes in v4:
time: 35.3 us; the launch traced here: 35.2 us
  Pallas kernels  14.1 us (40%)
  starting transfers between devices  13.6 us (39%)
  waiting for transfers between devices  7.36 us (21%)
    all_to_all x1, starting transfers between devices, local(): lax.all_to_all(outgoing, ('row', 'col'), split_axis=0, concat_axis=0, til...  7.89 us
    all_to_all x1, waiting for transfers between devices, local(): lax.all_to_all(outgoing, ('row', 'col'), split_axis=0, concat_axis=0, til...  7.35 us
    ppermute x1, starting transfers between devices, local(): second = lax.ppermute(charges, 'col', others + [(j, i) for i, j in others])  5.75 us
    pallas_call x1, Pallas kernels, local(): pl.pallas_call(project_kernel, out_shape=jax.ShapeDtypeStruct(message, jn...  5.65 us
    pallas_call x1, Pallas kernels, local(): pl.pallas_call(near_kernel, out_shape=(pltpu.HBM(charges.shape, jnp.float...  4.61 us
    pallas_call x1, Pallas kernels, local(): pl.pallas_call(far_kernel, out_shape=jax.ShapeDtypeStruct(charges.shape,...  3.87 us
  transfers between devices with their start and end apart: 3, of which 1 were waited for; matrix products, arithmetic and copies ran while one was open for 0% of the time, Pallas kernels for 29%

profile of v4, /device:TPU:1, one launch (start us, length us, event | category | flops | bytes accessed | tf_op | source)
XLA Modules:
  0.0 35.2 jit_solution(12097579671066282963)
XLA Ops:
  0.0 5.7 %collective-permute-start.1 = (bf16[2,48,1024]{2,1,0:T(8,128)(2,1)}, bf16[2,48,1024]{2,1,0:T(8,128)(2,1)S(1)}, u32[]{:S(2)}, u32[]{:S(2)}) collective-permute-start(bf16[2,48,1024]{2,1,0:T(8,128)(2,1)} %charges_hbm.1), channel_id=1, source_target_pairs={{1,2},{3,4},{5,6},{7,8},{9,10},{11,12},{13,14},{15,0},{2,1},{4,3},... | collective-permute-start | bytes 589832 | tf_op jit(solution)/shard_map/ppermute | solution.py:250
  5.7 0.0 collective-permute-start
  5.8 5.7 %project.1 = bf16[128,3,4,128]{3,2,1,0:T(4,128)(2,1)} custom-call(s32[128]{0:T(128)} %bitcast.8, s32[128]{0:T(128)} %bitcast.9, bf16[2,48,1024]{2,1,0:T(8,128)(2,1)} %charges_hbm.1, bf16[128,32,1024]{2,1,0:T(8,128)(2,1)} %bitcast.5), custom_call_target="tpu_custom_call" | custom-call | tf_op jit(solution)/shard_map/project/pallas_call | solution.py:251
  11.4 7.9 %all-to-all-start = ((bf16[128,3,4,128]{3,2,1,0:T(4,128)(2,1)}), bf16[128,3,4,128]{3,2,1,0:T(4,128)(2,1)S(1)}, u32[]{:S(2)}, u32[]{:S(2)}) async-start(bf16[128,3,4,128]{3,2,1,0:T(4,128)(2,1)} %project.1), calls=%async_computation | async-start | bytes 786432 | tf_op jit(solution)/shard_map/all_to_all | solution.py:274
  19.3 0.0 collective-permute-done.1.second_ref
  19.3 0.0 collective-permute-done.first_ref
  19.3 4.6 %near.1 = (f32[2,48,1024]{2,1,0:T(8,128)}, bf16[40,32,1024]{2,1,0:T(8,128)(2,1)S(1)}, f32[32,128]{1,0:T(8,128)S(1)}) custom-call(s32[2,2]{1,0:T(2,128)} %src_hbm.1, s32[128]{0:T(128)} %bitcast.10, bf16[2,48,1024]{2,1,0:T(8,128)(2,1)S(1)} %collective-permute-done.first_ref, bf16[2,48,1024]{2,1,0:T(8,128)(2,1)} %charges_hbm.1, ...), custom_call_target="tpu_custom_call" | custom-call | flops 20000000000 | bytes 10485760 | tf_op jit(solution)/shard_map/near/pallas_call | solution.py:276
  23.9 7.4 %all-to-all-done.in_ref = bf16[128,3,4,128]{3,2,1,0:T(4,128)(2,1)S(1)} async-done(((bf16[128,3,4,128]{3,2,1,0:T(4,128)(2,1)}), bf16[128,3,4,128]{3,2,1,0:T(4,128)(2,1)S(1)}, u32[]{:S(2)}, u32[]{:S(2)}) %all-to-all-start) | async-done | bytes 393248 | tf_op jit(solution)/shard_map/all_to_all | solution.py:274
  31.3 3.9 %far.1 = f32[2,48,1024]{2,1,0:T(8,128)} custom-call(f32[32,128]{1,0:T(8,128)S(1)} %get-tuple-element.8.lanes_ref, bf16[128,3,4,128]{3,2,1,0:T(4,128)(2,1)S(1)} %all-to-all-done.in_ref, bf16[40,32,1024]{2,1,0:T(8,128)(2,1)S(1)} %get-tuple-element.9.staged_ref, bf16[128,32,1024]{2,1,0:T(8,128)(2,1)} %bitcast.7, f32[2,48,1024]{2,1,0:T(8,128)} %get-tuple-element.10.near_hbm), custom_call_target="tpu_custom_call" | custom-call | tf_op jit(solution)/shard_map/far/pallas_call | solution.py:306
Async XLA Ops:
  0.0 19.3 %collective-permute-start.1 = (bf16[2,48,1024]{2,1,0:T(8,128)(2,1)}, bf16[2,48,1024]{2,1,0:T(8,128)(2,1)S(1)}, u32[]{:S(2)}, u32[]{:S(2)}) collective-permute-start(bf16[2,48,1024]{2,1,0:T(8,128)(2,1)} %charges_hbm.1), channel_id=1, source_target_pairs={{1,2},{3,4},{5,6},{7,8},{9,10},{11,12},{13,14},{15,0},{2,1},{4,3},... | collective-permute-start | bytes 589832 | tf_op jit(solution)/shard_map/ppermute | solution.py:250
  5.7 13.6 %collective-permute-start = (bf16[2,48,1024]{2,1,0:T(8,128)(2,1)}, bf16[2,48,1024]{2,1,0:T(8,128)(2,1)S(1)}, u32[]{:S(2)}, u32[]{:S(2)}) collective-permute-start(bf16[2,48,1024]{2,1,0:T(8,128)(2,1)} %charges_hbm.1), channel_id=1, source_target_pairs={{0,1},{2,3},{4,5},{6,7},{8,9},{10,11},{12,13},{14,15},{1,0},{3,2},... | collective-permute-start | bytes 589832 | tf_op jit(solution)/shard_map/ppermute | solution.py:249
  11.4 19.9 %all-to-all-start = ((bf16[128,3,4,128]{3,2,1,0:T(4,128)(2,1)}), bf16[128,3,4,128]{3,2,1,0:T(4,128)(2,1)S(1)}, u32[]{:S(2)}, u32[]{:S(2)}) async-start(bf16[128,3,4,128]{3,2,1,0:T(4,128)(2,1)} %project.1), calls=%async_computation | async-start | bytes 786432 | tf_op jit(solution)/shard_map/all_to_all | solution.py:274

commit v5 on v4

--- a/solution.py
+++ b/solution.py
@@ -177,8 +177,6 @@
 ):
     kept_blocks, width, elements = staged_ref.shape
     clusters, rhs, _ = total_ref.shape
-    fetch = pltpu.make_async_copy(near_hbm, near_ref, sems.at[len(U_SIZES)])
-    fetch.start()
     copies = []
     spans = [(0, kept_blocks, staged_ref, 0)]
     for chunk, at in enumerate(offsets(U_SIZES)):
@@ -187,6 +185,8 @@
         copies.append(pltpu.make_async_copy(source, u_ref.at[pl.ds(at, size)], sems.at[chunk]))
         copies[-1].start()
         spans.append((kept_blocks + at, size, u_ref, at))
+    fetch = pltpu.make_async_copy(near_hbm, near_ref, sems.at[len(U_SIZES)])
+    fetch.start()
     per = LANES // width
     parts = rhs // 16
 
@@ -207,8 +207,6 @@
     for index, (begin, size, ref, at) in enumerate(spans):
         if index:
             copies[index - 1].wait()
-        if index == 1:
-            fetch.wait()
         x = x_ref[:, begin * width : (begin + size) * width]
         final = index == len(spans) - 1
         for half in range(HALVES):
@@ -218,7 +216,9 @@
             part = part.reshape(clusters, rhs, elements // HALVES)
             if index:
                 part += total_ref[:, :, columns]
-            if index == 1:
+            if final:
+                if half == 0:
+                    fetch.wait()
                 part += near_ref[:, :, columns]
             total_ref[:, :, columns] = part
             if final:

time: 35.3 us -> 35.2 us (level)
  no operation moved by 1% of the time
where the time goes in v5:
time: 35.2 us; the launch traced here: 35.1 us
  Pallas kernels  14 us (40%)
  starting transfers between devices  13.6 us (39%)
  waiting for transfers between devices  7.36 us (21%)
    all_to_all x1, starting transfers between devices, local(): lax.all_to_all(outgoing, ('row', 'col'), split_axis=0, concat_axis=0, til...  7.89 us
    all_to_all x1, waiting for transfers between devices, local(): lax.all_to_all(outgoing, ('row', 'col'), split_axis=0, concat_axis=0, til...  7.35 us
    ppermute x1, starting transfers between devices, local(): second = lax.ppermute(charges, 'col', others + [(j, i) for i, j in others])  5.75 us
    pallas_call x1, Pallas kernels, local(): pl.pallas_call(project_kernel, out_shape=jax.ShapeDtypeStruct(message, jn...  5.65 us
    pallas_call x1, Pallas kernels, local(): pl.pallas_call(near_kernel, out_shape=(pltpu.HBM(charges.shape, jnp.float...  4.61 us
    pallas_call x1, Pallas kernels, local(): pl.pallas_call(far_kernel, out_shape=jax.ShapeDtypeStruct(charges.shape,...  3.77 us
  transfers between devices with their start and end apart: 3, of which 1 were waited for; matrix products, arithmetic and copies ran while one was open for 0% of the time, Pallas kernels for 29%

profile of v5, /device:TPU:1, one launch (start us, length us, event | category | flops | bytes accessed | tf_op | source)
XLA Modules:
  0.0 35.1 jit_solution(93405578025830346)
XLA Ops:
  0.0 5.7 %collective-permute-start.1 = (bf16[2,48,1024]{2,1,0:T(8,128)(2,1)}, bf16[2,48,1024]{2,1,0:T(8,128)(2,1)S(1)}, u32[]{:S(2)}, u32[]{:S(2)}) collective-permute-start(bf16[2,48,1024]{2,1,0:T(8,128)(2,1)} %charges_hbm.1), channel_id=1, source_target_pairs={{1,2},{3,4},{5,6},{7,8},{9,10},{11,12},{13,14},{15,0},{2,1},{4,3},... | collective-permute-start | bytes 589832 | tf_op jit(solution)/shard_map/ppermute | solution.py:250
  5.7 0.0 collective-permute-start
  5.8 5.7 %project.1 = bf16[128,3,4,128]{3,2,1,0:T(4,128)(2,1)} custom-call(s32[128]{0:T(128)} %bitcast.8, s32[128]{0:T(128)} %bitcast.9, bf16[2,48,1024]{2,1,0:T(8,128)(2,1)} %charges_hbm.1, bf16[128,32,1024]{2,1,0:T(8,128)(2,1)} %bitcast.5), custom_call_target="tpu_custom_call" | custom-call | tf_op jit(solution)/shard_map/project/pallas_call | solution.py:251
  11.4 7.9 %all-to-all-start = ((bf16[128,3,4,128]{3,2,1,0:T(4,128)(2,1)}), bf16[128,3,4,128]{3,2,1,0:T(4,128)(2,1)S(1)}, u32[]{:S(2)}, u32[]{:S(2)}) async-start(bf16[128,3,4,128]{3,2,1,0:T(4,128)(2,1)} %project.1), calls=%async_computation | async-start | bytes 786432 | tf_op jit(solution)/shard_map/all_to_all | solution.py:274
  19.3 0.0 collective-permute-done.1.second_ref
  19.3 0.0 collective-permute-done.first_ref
  19.3 4.6 %near.1 = (f32[2,48,1024]{2,1,0:T(8,128)}, bf16[40,32,1024]{2,1,0:T(8,128)(2,1)S(1)}, f32[32,128]{1,0:T(8,128)S(1)}) custom-call(s32[2,2]{1,0:T(2,128)} %src_hbm.1, s32[128]{0:T(128)} %bitcast.10, bf16[2,48,1024]{2,1,0:T(8,128)(2,1)S(1)} %collective-permute-done.first_ref, bf16[2,48,1024]{2,1,0:T(8,128)(2,1)} %charges_hbm.1, ...), custom_call_target="tpu_custom_call" | custom-call | flops 20000000000 | bytes 10485760 | tf_op jit(solution)/shard_map/near/pallas_call | solution.py:276
  23.9 7.4 %all-to-all-done.in_ref = bf16[128,3,4,128]{3,2,1,0:T(4,128)(2,1)S(1)} async-done(((bf16[128,3,4,128]{3,2,1,0:T(4,128)(2,1)}), bf16[128,3,4,128]{3,2,1,0:T(4,128)(2,1)S(1)}, u32[]{:S(2)}, u32[]{:S(2)}) %all-to-all-start) | async-done | bytes 393248 | tf_op jit(solution)/shard_map/all_to_all | solution.py:274
  31.3 3.8 %far.1 = f32[2,48,1024]{2,1,0:T(8,128)} custom-call(f32[32,128]{1,0:T(8,128)S(1)} %get-tuple-element.8.lanes_ref, bf16[128,3,4,128]{3,2,1,0:T(4,128)(2,1)S(1)} %all-to-all-done.in_ref, bf16[40,32,1024]{2,1,0:T(8,128)(2,1)S(1)} %get-tuple-element.9.staged_ref, bf16[128,32,1024]{2,1,0:T(8,128)(2,1)} %bitcast.7, f32[2,48,1024]{2,1,0:T(8,128)} %get-tuple-element.10.near_hbm), custom_call_target="tpu_custom_call" | custom-call | tf_op jit(solution)/shard_map/far/pallas_call | solution.py:306
Async XLA Ops:
  0.0 19.3 %collective-permute-start.1 = (bf16[2,48,1024]{2,1,0:T(8,128)(2,1)}, bf16[2,48,1024]{2,1,0:T(8,128)(2,1)S(1)}, u32[]{:S(2)}, u32[]{:S(2)}) collective-permute-start(bf16[2,48,1024]{2,1,0:T(8,128)(2,1)} %charges_hbm.1), channel_id=1, source_target_pairs={{1,2},{3,4},{5,6},{7,8},{9,10},{11,12},{13,14},{15,0},{2,1},{4,3},... | collective-permute-start | bytes 589832 | tf_op jit(solution)/shard_map/ppermute | solution.py:250
  5.7 13.6 %collective-permute-start = (bf16[2,48,1024]{2,1,0:T(8,128)(2,1)}, bf16[2,48,1024]{2,1,0:T(8,128)(2,1)S(1)}, u32[]{:S(2)}, u32[]{:S(2)}) collective-permute-start(bf16[2,48,1024]{2,1,0:T(8,128)(2,1)} %charges_hbm.1), channel_id=1, source_target_pairs={{0,1},{2,3},{4,5},{6,7},{8,9},{10,11},{12,13},{14,15},{1,0},{3,2},... | collective-permute-start | bytes 589832 | tf_op jit(solution)/shard_map/ppermute | solution.py:249
  11.4 19.9 %all-to-all-start = ((bf16[128,3,4,128]{3,2,1,0:T(4,128)(2,1)}), bf16[128,3,4,128]{3,2,1,0:T(4,128)(2,1)S(1)}, u32[]{:S(2)}, u32[]{:S(2)}) async-start(bf16[128,3,4,128]{3,2,1,0:T(4,128)(2,1)} %project.1), calls=%async_computation | async-start | bytes 786432 | tf_op jit(solution)/shard_map/all_to_all | solution.py:274
